TPU v7x, 512 devices: a whole 4x8x8 slice. The times are simulated.
512 devices in a mesh: coil: 32 (over x, z), frame: 16 (over y, core).
Axes of the slice: x: 4, y: 8, z: 8, core: 2. Of those that a mesh axis runs over, the one named last changes fastest.
Arguments:
- initial_image: float32 [256, 16, 2, 256], P('coil', 'frame'), may hold values from -3 to 3
- coil_maps: bfloat16 [32, 2, 256, 256], P('coil'), may hold values from -1.5 to 1.5
- samples: bfloat16 [32, 16, 18, 2, 256], P('coil', 'frame'), may hold values from -6 to 6
- blocks_used: int32 [16], P('frame'), may hold values from 1 to 18, 145 in all
- row_offset: int32 [16, 18], P('frame'), may hold values from 0 to 128
- col_offset: int32 [16, 18], P('frame'), may hold values from 0 to 128
- row_first: int32 [16, 18, 256], P('frame'), may hold values from 0 to 124
- col_first: int32 [16, 18, 256], P('frame'), may hold values from 0 to 124
- row_taps: bfloat16 [16, 18, 4, 256], P('frame'), may hold values from 0.099609375 to 0.59765625
- col_taps: bfloat16 [16, 18, 4, 256], P('frame'), may hold values from 0.099609375 to 0.59765625
Outputs:
- image: float32 [256, 16, 2, 256], P('coil', 'frame')
- misfit: float32 [2, 16], P(None, 'frame')
Inputs may be any that keep to these rules, and one draw needn't show every extreme that they name: Blocks 0 to blocks_used minus one of the frame were acquired. `row_first`: the kernel's 4 rows lie inside the tile. `col_first`: the kernel's 4 columns lie inside the tile.
All inputs are finite; a program needn't handle non-finite values.
Results may differ from a plain program's by a relative error of at most 0.006.
Values may be sent and summed in bfloat16 or wider, within the bound.
A program may use at most 64 MiB of HBM per device.

v0:
```python
import functools
import math

import jax
import jax.numpy as jnp
import numpy as np
from jax import lax
from jax.experimental import pallas as pl
from jax.experimental.pallas import tpu as pltpu
from jax.sharding import PartitionSpec as P

N = 256
NB = 18
BS = 256
KW = 4
ITERS = 2

step_size = 2.0
tv_weight = 0.1
smooth_floor = 0.5
shrink_weight = 0.1

MESH = pl.DeviceIdType.MESH
F32 = jnp.float32
BF16 = jnp.bfloat16


def dft_tables():
    counter = np.arange(N)
    angle = (counter[:, None] * counter[None, :] % N) * (2.0 * math.pi / N)
    cosine = jnp.asarray((np.cos(angle) / math.sqrt(N)).astype(np.float32)).astype(BF16)
    sine = jnp.asarray((np.sin(angle) / math.sqrt(N)).astype(np.float32)).astype(BF16)
    return np.stack([np.asarray(cosine), np.asarray(sine), np.asarray(-sine)])


def mm(a, b):
    return jnp.dot(a, b, preferred_element_type=F32)


def mm_nt(a, b):
    return lax.dot_general(a, b, (((1,), (1,)), ((), ())), preferred_element_type=F32)


def taps_of(first, offset, taps):
    distance = lax.broadcasted_iota(jnp.int32, (N, BS), 0) - (first + offset)
    matrix = jnp.zeros((N, BS), F32)
    for tap in range(KW):
        matrix = jnp.where(distance == tap, taps[tap : tap + 1, :], matrix)
    return matrix.astype(BF16)


def swap_lanes(field):
    lane = lax.broadcasted_iota(jnp.int32, field.shape, 1)
    width = field.shape[1]
    return jnp.where(
        lane % 2 == 0, pltpu.roll(field, width - 1, 1), pltpu.roll(field, 1, 1)
    )


def swap_rows(field):
    row = lax.broadcasted_iota(jnp.int32, field.shape, 0)
    height = field.shape[0]
    return jnp.where(
        row % 2 == 0, pltpu.roll(field, height - 1, 0), pltpu.roll(field, 1, 0)
    )


def shrunk(real, imag, limit):
    length = jnp.sqrt(real * real + imag * imag)
    factor = jnp.maximum(length - limit, 0.0) / jnp.maximum(length, limit)
    return real * factor, imag * factor


def wavelet_prox(real, imag, limit):
    parts = []
    for field in (real, imag):
        across = swap_lanes(field)
        down = swap_rows(field)
        both = swap_lanes(down)
        parts.append(
            (
                (field + across + down + both) * 0.5,
                (field - across + down - both) * 0.5,
                (field + across - down - both) * 0.5,
                (field - across - down + both) * 0.5,
            )
        )
    out_real, out_imag = parts[0][0], parts[1][0]
    for band in range(1, 4):
        band_real, band_imag = shrunk(parts[0][band], parts[1][band], limit)
        out_real = out_real + band_real
        out_imag = out_imag + band_imag
    return out_real * 0.5, out_imag * 0.5


def slope(late, early):
    real = late[0] - early[0]
    imag = late[1] - early[1]
    length = jnp.sqrt(real * real + imag * imag + smooth_floor * smooth_floor)
    return real / length, imag / length


def kernel(
    coils,
    frames,
    image_ref,
    maps_ref,
    samples_ref,
    used_ref,
    row_off_ref,
    col_off_ref,
    row_first_ref,
    col_first_ref,
    row_taps_ref,
    col_taps_ref,
    table_ref,
    out_ref,
    misfit_ref,
    current,
    low,
    gathered,
    beside,
    part_out,
    part_in,
    mis_out,
    mis_in,
    wx,
    wy,
    kspace,
    grid,
    send_sem,
    recv_sem,
    side_send,
    side_recv,
):
    me = lax.axis_index("coil")
    frame = lax.axis_index("frame")
    after = lax.rem(frame + 1, frames)
    before = lax.rem(frame + frames - 1, frames)

    def peer_of(k):
        return lax.rem(me + k, coils)

    barrier = pltpu.get_barrier_semaphore()

    def greet(k, carry):
        pl.semaphore_signal(
            barrier, inc=1, device_id={"coil": peer_of(k)}, device_id_type=MESH
        )
        return carry

    lax.fori_loop(1, coils, greet, 0)
    for side in (after, before):
        pl.semaphore_signal(barrier, inc=1, device_id={"frame": side}, device_id_type=MESH)

    for part in range(2):
        current[0, part] = image_ref[:, part, :]

    def build(b, carry):
        row_taps = row_taps_ref[b].astype(F32)
        col_taps = col_taps_ref[b].astype(F32)
        wx[b] = taps_of(row_first_ref[pl.ds(b, 1), :], row_off_ref[0, b], row_taps)
        wy[b] = taps_of(col_first_ref[pl.ds(b, 1), :], col_off_ref[0, b], col_taps)
        return carry

    def to_all(phase, source, target):
        def copy_of(k):
            peer = peer_of(k)
            return pltpu.make_async_remote_copy(
                src_ref=source(peer),
                dst_ref=target(me),
                send_sem=send_sem.at[phase, k],
                recv_sem=recv_sem.at[phase, k],
                device_id={"coil": peer},
                device_id_type=MESH,
            )

        def start(k, carry):
            copy_of(k).start()
            return carry

        def arrive(k, carry):
            copy_of(k).wait_recv()
            return carry

        def leave(k, carry):
            copy_of(k).wait_send()
            return carry

        lax.fori_loop(1, coils, start, 0)
        return (
            lambda: lax.fori_loop(1, coils, arrive, 0),
            lambda: lax.fori_loop(1, coils, leave, 0),
        )

    pl.semaphore_wait(barrier, coils + 1)
    leaving = []
    for step in range(ITERS):
        low[step] = current[step].astype(BF16)
        arrived, left = to_all(
            2 * step, lambda peer: low.at[step], lambda own: gathered.at[step, own]
        )
        leaving.append(left)
        sides = []
        for slot, side in ((0, after), (1, before)):
            copy = pltpu.make_async_remote_copy(
                src_ref=current.at[step],
                dst_ref=beside.at[step, slot],
                send_sem=side_send.at[step, slot],
                recv_sem=side_recv.at[step, slot],
                device_id={"frame": side},
                device_id_type=MESH,
            )
            copy.start()
            sides.append(copy)
        gathered[step, me] = low[step]
        if step == 0:
            lax.fori_loop(0, NB, build, 0)
        arrived()

        cosine, sine, minus = table_ref[0], table_ref[1], table_ref[2]
        map_real = maps_ref[0].astype(F32)
        map_imag = maps_ref[1].astype(F32)
        image_real = gathered[step, :, 0].astype(F32).reshape(N, N)
        image_imag = gathered[step, :, 1].astype(F32).reshape(N, N)
        coil_real = (map_real * image_real - map_imag * image_imag).astype(BF16)
        coil_imag = (map_real * image_imag + map_imag * image_real).astype(BF16)
        half_real = (mm(cosine, coil_real) + mm(sine, coil_imag)).astype(BF16)
        half_imag = (mm(cosine, coil_imag) + mm(minus, coil_real)).astype(BF16)
        kspace[0:N] = (mm(half_real, cosine) + mm(half_imag, sine)).astype(BF16)
        kspace[N : 2 * N] = (mm(half_imag, cosine) + mm(half_real, minus)).astype(BF16)

        grid[...] = jnp.zeros_like(grid)

        def visit(b, misfit):
            across = mm(kspace[...], wy[b])
            rows = wx[b].astype(F32)
            measured = samples_ref[b].astype(F32)
            active = jnp.full((1, BS), b, jnp.int32) < used_ref[0]
            spread = []
            for part in range(2):
                predicted = jnp.sum(across[part * N : part * N + N] * rows, axis=0, keepdims=True)
                resid = jnp.where(active, predicted - measured[part : part + 1], 0.0)
                misfit = misfit + resid * resid
                spread.append((resid.astype(BF16).astype(F32) * rows).astype(BF16))
            grid[...] += mm_nt(jnp.concatenate(spread, axis=0), wy[b])
            return misfit

        misfit = lax.fori_loop(0, NB, visit, jnp.zeros((1, BS), F32))
        mis_out[step : step + 1, :] = misfit

        if step == ITERS - 1:
            all_misfit, left = to_all(
                2 * ITERS, lambda peer: mis_out, lambda own: mis_in.at[own]
            )
            leaving.append(left)
            mis_in[me] = mis_out[...]

        grid_real = grid[0:N].astype(BF16)
        grid_imag = grid[N : 2 * N].astype(BF16)
        back_real = (mm(cosine, grid_real) + mm(minus, grid_imag)).astype(BF16)
        back_imag = (mm(cosine, grid_imag) + mm(sine, grid_real)).astype(BF16)
        coil_real = mm(back_real, cosine) + mm(back_imag, minus)
        coil_imag = mm(back_imag, cosine) + mm(back_real, sine)
        height = N // coils
        part_out[step, :, 0] = (
            (map_real * coil_real + map_imag * coil_imag).reshape(coils, height, N).astype(BF16)
        )
        part_out[step, :, 1] = (
            (map_real * coil_imag - map_imag * coil_real).reshape(coils, height, N).astype(BF16)
        )
        arrived, left = to_all(
            2 * step + 1,
            lambda peer: part_out.at[step, peer],
            lambda own: part_in.at[step, own],
        )
        leaving.append(left)
        part_in[step, me] = part_out[step, me]
        for copy in sides:
            copy.wait()
        here = (current[step, 0], current[step, 1])
        early = (beside[step, 0, 0], beside[step, 0, 1])
        late = (beside[step, 1, 0], beside[step, 1, 1])
        first = slope(here, early)
        second = slope(late, here)
        arrived()
        result = []
        for part in range(2):
            gradient = jnp.sum(part_in[step, :, part].astype(F32), axis=0)
            result.append(
                here[part] - step_size * (gradient + tv_weight * (first[part] - second[part]))
            )
        result = wavelet_prox(result[0], result[1], step_size * shrink_weight)
        if step < ITERS - 1:
            for part in range(2):
                current[step + 1, part] = result[part]
        else:
            for part in range(2):
                out_ref[:, part, :] = result[part]

    all_misfit()
    total = jnp.sum(mis_in[...], axis=0)
    total = jnp.sum(total, axis=1, keepdims=True) * (0.5 / (coils * NB * BS))
    misfit_ref[...] = jnp.broadcast_to(total, misfit_ref.shape)
    for left in leaving:
        left()


def solution(mesh):
    coils = mesh.shape["coil"]
    frames = mesh.shape["frame"]
    height = N // coils
    tables = dft_tables()
    vmem = pl.BlockSpec(memory_space=pltpu.VMEM)
    smem = pl.BlockSpec(memory_space=pltpu.SMEM)

    def on_device(
        initial_image,
        coil_maps,
        samples,
        blocks_used,
        row_offset,
        col_offset,
        row_first,
        col_first,
        row_taps,
        col_taps,
    ):
        image, misfit = pl.pallas_call(
            functools.partial(kernel, coils, frames),
            out_shape=(
                jax.ShapeDtypeStruct((height, 2, N), F32),
                jax.ShapeDtypeStruct((ITERS, 128), F32),
            ),
            in_specs=[vmem, vmem, vmem, smem, smem, smem, vmem, vmem, vmem, vmem, vmem],
            out_specs=(vmem, vmem),
            scratch_shapes=[
                pltpu.VMEM((ITERS, 2, height, N), F32),
                pltpu.VMEM((ITERS, 2, height, N), BF16),
                pltpu.VMEM((ITERS, coils, 2, height, N), BF16),
                pltpu.VMEM((ITERS, 2, 2, height, N), F32),
                pltpu.VMEM((ITERS, coils, 2, height, N), BF16),
                pltpu.VMEM((ITERS, coils, 2, height, N), BF16),
                pltpu.VMEM((ITERS, BS), F32),
                pltpu.VMEM((coils, ITERS, BS), F32),
                pltpu.VMEM((NB, N, BS), BF16),
                pltpu.VMEM((NB, N, BS), BF16),
                pltpu.VMEM((2 * N, N), BF16),
                pltpu.VMEM((2 * N, N), F32),
                pltpu.SemaphoreType.DMA((2 * ITERS + 1, coils)),
                pltpu.SemaphoreType.DMA((2 * ITERS + 1, coils)),
                pltpu.SemaphoreType.DMA((ITERS, 2)),
                pltpu.SemaphoreType.DMA((ITERS, 2)),
            ],
            compiler_params=pltpu.CompilerParams(
                collective_id=0, has_side_effects=True, vmem_limit_bytes=40 * 1024 * 1024
            ),
        )(
            initial_image[:, 0],
            coil_maps[0],
            samples[0, 0],
            blocks_used,
            row_offset,
            col_offset,
            row_first[0],
            col_first[0],
            row_taps[0],
            col_taps[0],
            tables,
        )
        return image[:, None], misfit[:, :1]

    placed = (
        P("coil", "frame", None, None),
        P("coil", None, None, None),
        P("coil", "frame", None, None, None),
        P("frame"),
        P("frame", None),
        P("frame", None),
        P("frame", None, None),
        P("frame", None, None),
        P("frame", None, None, None),
        P("frame", None, None, None),
    )
    return jax.shard_map(
        on_device,
        mesh=mesh,
        in_specs=placed,
        out_specs=(P("coil", "frame", None, None), P(None, "frame")),
        check_vma=False,
    )
```

profile of v0, /device:TPU:32, one launch (start us, length us, event | category | flops | bytes accessed | tf_op | source)
XLA Modules:
  0.0 80.4 jit_solution(16004359530561809193)
XLA Ops:
  1.3 0.0 copy-start.4
  1.3 0.0 copy-start.2
  1.3 0.0 copy-start.3
  1.3 0.8 copy_bitcast_fusion
  2.1 0.0 copy-start.6
  2.1 0.0 copy-start.7
  2.1 0.0 copy-done.4
  2.1 0.0 copy-done.2
  2.1 0.0 copy-done.3
  2.1 0.6 copy-done.6
  2.7 0.0 copy-done.7
  2.7 0.0 copy-start
  2.7 1.0 %copy-done = bf16[3,256,256]{2,1,0:T(8,128)(2,1)S(1)} copy-done((bf16[3,256,256]{2,1,0:T(8,128)(2,1)S(1)}, bf16[3,256,256]{2,1,0:T(8,128)(2,1)}, u32[]{:S(2)}) %copy-start) | copy-done | bytes 393240
  3.7 0.0 copy-start.1
  3.7 0.9 %copy-done.1 = bf16[1,2,256,256]{3,2,1,0:T(8,128)(2,1)S(1)} copy-done((bf16[1,2,256,256]{3,2,1,0:T(8,128)(2,1)S(1)}, bf16[1,2,256,256]{3,2,1,0:T(8,128)(2,1)}, u32[]{:S(2)}) %copy-start.1) | copy-done | bytes 262168
  4.7 0.0 copy-start.5
  4.7 0.7 copy-done.5
  5.4 73.8 %shard_map.122 = (f32[8,2,256]{2,1,0:T(2,128)S(1)}, f32[2,128]{1,0:T(2,128)S(1)}) custom-call(f32[8,2,256]{2,1,0:T(2,128)S(1)} %bitcast.17, bf16[2,256,256]{2,1,0:T(8,128)(2,1)S(1)} %bitcast.13, bf16[18,2,256]{2,1,0:T(2,128)(2,1)S(1)} %bitcast.16, s32[1]{0:T(128)S(6)} %copy.20.used_ref, s32[1,18]{1,0:T(1,128)S(1)} %copy-done.6, s32[1,18]{1,0:T(1,128)S(1)} %copy-done.7, ...), custom_call_target="tpu_custom_call" | custom-call | tf_op jit(solution)/shard_map/pallas_call | solution.py:329
  79.2 0.6 copy.14
  79.8 0.6 copy.21
Async XLA Ops:
  1.3 0.8 copy-start.4
  1.3 0.8 copy-start.2
  1.3 0.8 copy-start.3
  2.1 0.7 copy-start.6
  2.1 0.7 copy-start.7
  2.7 1.0 %copy-start = (bf16[3,256,256]{2,1,0:T(8,128)(2,1)S(1)}, bf16[3,256,256]{2,1,0:T(8,128)(2,1)}, u32[]{:S(2)}) copy-start(bf16[3,256,256]{2,1,0:T(8,128)(2,1)} %constant.2.clone.table_ref) | copy-start | bytes 1179652
  3.7 0.9 %copy-start.1 = (bf16[1,2,256,256]{3,2,1,0:T(8,128)(2,1)S(1)}, bf16[1,2,256,256]{3,2,1,0:T(8,128)(2,1)}, u32[]{:S(2)}) copy-start(bf16[1,2,256,256]{3,2,1,0:T(8,128)(2,1)} %param.12) | copy-start | bytes 786436
  4.7 0.7 copy-start.5
where the time goes:
time: 80.7 us; the launch traced here: 80.4 us
  Pallas kernels  73.8 us (91%)
  local copies, waits for them, and re-layouts  5.28 us (7%)
  between operations  1.34 us (2%)
    pallas_call x1, Pallas kernels, on_device(): pl.pallas_call(functools.partial(kernel, coils, frames), out_shape=(jax.S...  73.8 us
    unnamed x19, local copies, waits for them, and re-layouts  5.28 us

commit v1 on v0

v1 whole, which is shorter than its diff:
```python
import functools
import math

import jax
import jax.numpy as jnp
import numpy as np
from jax import lax
from jax.experimental import pallas as pl
from jax.experimental.pallas import tpu as pltpu
from jax.sharding import PartitionSpec as P

N = 256
NB = 18
BS = 256
KW = 4
ITERS = 2

step_size = 2.0
tv_weight = 0.1
smooth_floor = 0.5
shrink_weight = 0.1

RING = 8
RING_FAR = (4, 3, 5, 2, 6, 1, 7)
CROSS_FAR = (2, 1, 3)
GROUP = 6

MESH = pl.DeviceIdType.MESH
F32 = jnp.float32
BF16 = jnp.bfloat16


def dft_tables():
    counter = np.arange(N)
    angle = (counter[:, None] * counter[None, :] % N) * (2.0 * math.pi / N)
    cosine = jnp.asarray((np.cos(angle) / math.sqrt(N)).astype(np.float32)).astype(BF16)
    sine = jnp.asarray((np.sin(angle) / math.sqrt(N)).astype(np.float32)).astype(BF16)
    return np.stack([np.asarray(cosine), np.asarray(sine), np.asarray(-sine)])


def mm(a, b):
    return jnp.dot(a, b, preferred_element_type=F32)


def mm_nt(a, b):
    return lax.dot_general(a, b, (((1,), (1,)), ((), ())), preferred_element_type=F32)


def taps_of(first, offset, taps):
    distance = lax.broadcasted_iota(jnp.int32, (N, BS), 0) - (first + offset)
    matrix = jnp.zeros((N, BS), F32)
    for tap in range(KW):
        matrix = jnp.where(distance == tap, taps[tap : tap + 1, :], matrix)
    return matrix.astype(BF16)


def swap_lanes(field):
    lane = lax.broadcasted_iota(jnp.int32, field.shape, 1)
    width = field.shape[1]
    return jnp.where(
        lane % 2 == 0, pltpu.roll(field, width - 1, 1), pltpu.roll(field, 1, 1)
    )


def swap_rows(field):
    row = lax.broadcasted_iota(jnp.int32, field.shape, 0)
    height = field.shape[0]
    return jnp.where(
        row % 2 == 0, pltpu.roll(field, height - 1, 0), pltpu.roll(field, 1, 0)
    )


def shrunk(real, imag, limit):
    length = jnp.sqrt(real * real + imag * imag)
    factor = jnp.maximum(length - limit, 0.0) / jnp.maximum(length, limit)
    return real * factor, imag * factor


def wavelet_prox(real, imag, limit):
    parts = []
    for field in (real, imag):
        across = swap_lanes(field)
        down = swap_rows(field)
        both = swap_lanes(down)
        parts.append(
            (
                (field + across + down + both) * 0.5,
                (field - across + down - both) * 0.5,
                (field + across - down - both) * 0.5,
                (field - across - down + both) * 0.5,
            )
        )
    out_real, out_imag = parts[0][0], parts[1][0]
    for band in range(1, 4):
        band_real, band_imag = shrunk(parts[0][band], parts[1][band], limit)
        out_real = out_real + band_real
        out_imag = out_imag + band_imag
    return out_real * 0.5, out_imag * 0.5


def slope(late, early):
    real = late[0] - early[0]
    imag = late[1] - early[1]
    length = jnp.sqrt(real * real + imag * imag + smooth_floor * smooth_floor)
    return real / length, imag / length


def kernel(
    coils,
    frames,
    image_hbm,
    maps_hbm,
    samples_hbm,
    used_hbm,
    row_off_hbm,
    col_off_hbm,
    row_first_hbm,
    col_first_hbm,
    row_taps_hbm,
    col_taps_hbm,
    table_hbm,
    out_ref,
    misfit_ref,
    image_ref,
    maps_ref,
    samples_ref,
    used_ref,
    row_off_ref,
    col_off_ref,
    row_first_ref,
    col_first_ref,
    row_taps_ref,
    col_taps_ref,
    table_ref,
    current,
    low,
    gathered,
    beside,
    adjoint,
    part_out,
    part_in,
    mid_out,
    mid_in,
    mis_out,
    mis_in,
    mis_mid,
    mis_end,
    wx,
    wy,
    kspace,
    weighted,
    local_sem,
    ring_send,
    ring_recv,
    cross_send,
    cross_recv,
    side_send,
    side_recv,
    mis_send,
    mis_recv,
):
    me = lax.axis_index("coil")
    frame = lax.axis_index("frame")
    columns = coils // RING
    my_z = lax.rem(me, RING)
    my_x = me // RING
    height = N // coils

    def ring_coil(k):
        return my_x * RING + lax.rem(my_z + k, RING)

    def cross_x(k):
        return lax.rem(my_x + k, columns)

    def cross_coil(k):
        return cross_x(k) * RING + my_z

    after = lax.rem(frame + 1, frames)
    before = lax.rem(frame + frames - 1, frames)

    fetches = []
    for slot, (source, target) in enumerate(
        (
            (image_hbm, image_ref),
            (row_off_hbm, row_off_ref),
            (row_first_hbm, row_first_ref),
            (row_taps_hbm, row_taps_ref),
            (col_off_hbm, col_off_ref),
            (col_first_hbm, col_first_ref),
            (col_taps_hbm, col_taps_ref),
            (maps_hbm, maps_ref),
            (table_hbm, table_ref),
            (samples_hbm, samples_ref),
            (used_hbm, used_ref),
        )
    ):
        fetch = pltpu.make_async_copy(source, target, local_sem.at[slot])
        fetch.start()
        fetches.append(fetch)

    barrier = pltpu.get_barrier_semaphore()
    for k in RING_FAR:
        pl.semaphore_signal(
            barrier, inc=1, device_id={"coil": ring_coil(k)}, device_id_type=MESH
        )
    for k in CROSS_FAR:
        pl.semaphore_signal(
            barrier, inc=1, device_id={"coil": cross_coil(k)}, device_id_type=MESH
        )
    for side in (after, before):
        pl.semaphore_signal(barrier, inc=1, device_id={"frame": side}, device_id_type=MESH)

    leaving = []

    def send(source, target, send_sem, recv_sem, device):
        copy = pltpu.make_async_remote_copy(
            src_ref=source,
            dst_ref=target,
            send_sem=send_sem,
            recv_sem=recv_sem,
            device_id=device,
            device_id_type=MESH,
        )
        copy.start()
        leaving.append(copy)
        return copy

    fetches[0].wait()
    for part in range(2):
        current[0, part] = image_ref[:, part, :]
        low[0, part] = image_ref[:, part, :].astype(BF16)

    def build(first_ref, off_ref, taps_ref, out, b, carry):
        out[b] = taps_of(first_ref[b], off_ref[0, b], taps_ref[b].astype(F32))
        return carry

    for fetch in fetches[1:4]:
        fetch.wait()
    lax.fori_loop(
        0, NB, functools.partial(build, row_first_ref, row_off_ref, row_taps_ref, wx), 0
    )
    pl.semaphore_wait(barrier, RING - 1 + columns - 1 + 2)

    for step in range(ITERS):
        sides = [
            send(
                current.at[step],
                beside.at[step, slot],
                side_send.at[step, slot],
                side_recv.at[step, slot],
                {"frame": side},
            )
            for slot, side in ((0, after), (1, before))
        ]
        ring = {}
        cross = {}
        for k in RING_FAR:
            ring[k] = send(
                low.at[step],
                gathered.at[step, me],
                ring_send.at[2 * step, k],
                ring_recv.at[2 * step, k],
                {"coil": ring_coil(k)},
            )

        def forward(k, source):
            for far in CROSS_FAR:
                cross[far, k] = send(
                    source,
                    gathered.at[step, my_x * RING + lax.rem(my_z + RING - k, RING)],
                    cross_send.at[2 * step, far, k],
                    cross_recv.at[2 * step, far, k],
                    {"coil": cross_coil(far)},
                )

        forward(0, low.at[step])
        gathered[step, me] = low[step]
        if step == 0:
            for fetch in fetches[4:7]:
                fetch.wait()
            lax.fori_loop(
                0, NB, functools.partial(build, col_first_ref, col_off_ref, col_taps_ref, wy), 0
            )
            for fetch in fetches[7:]:
                fetch.wait()
        for k in reversed(RING_FAR):
            ring[k].wait_recv()
            forward(k, gathered.at[step, my_x * RING + lax.rem(my_z + RING - k, RING)])
        for copy in cross.values():
            copy.wait_recv()

        cosine, sine, minus = table_ref[0], table_ref[1], table_ref[2]
        map_real = maps_ref[0].astype(F32)
        map_imag = maps_ref[1].astype(F32)
        image_real = gathered[step, :, 0].astype(F32).reshape(N, N)
        image_imag = gathered[step, :, 1].astype(F32).reshape(N, N)
        coil_real = (map_real * image_real - map_imag * image_imag).astype(BF16)
        coil_imag = (map_real * image_imag + map_imag * image_real).astype(BF16)
        half_real = (mm(cosine, coil_real) + mm(sine, coil_imag)).astype(BF16)
        half_imag = (mm(cosine, coil_imag) + mm(minus, coil_real)).astype(BF16)
        kspace[0:N] = (mm(half_real, cosine) + mm(half_imag, sine)).astype(BF16)
        kspace[N : 2 * N] = (mm(half_imag, cosine) + mm(half_real, minus)).astype(BF16)

        def visit(b, misfit):
            across = mm(kspace[...], wy[b])
            rows = wx[b]
            wide = rows.astype(F32)
            measured = samples_ref[b].astype(F32)
            active = jnp.full((1, BS), b, jnp.int32) < used_ref[0]
            for part in range(2):
                predicted = jnp.sum(across[part * N : part * N + N] * wide, axis=0, keepdims=True)
                resid = jnp.where(active, predicted - measured[part : part + 1], 0.0)
                misfit = misfit + resid * resid
                weighted[b, part * N : part * N + N] = resid.astype(BF16) * rows
            return misfit

        def visits(group, misfit):
            for b in range(GROUP):
                misfit = visit(group * GROUP + b, misfit)
            return misfit

        misfit = lax.fori_loop(0, NB // GROUP, visits, jnp.zeros((1, BS), F32))
        mis_out[step : step + 1, :] = misfit

        if step == ITERS - 1:
            mis_cross = [
                send(
                    mis_out,
                    mis_in.at[far],
                    mis_send.at[0, far],
                    mis_recv.at[0, far],
                    {"coil": cross_coil(far)},
                )
                for far in CROSS_FAR
            ]

        total = mm_nt(weighted[0], wy[0])
        for b in range(1, NB):
            total = total + mm_nt(weighted[b], wy[b])
        grid_real = total[0:N].astype(BF16)
        grid_imag = total[N : 2 * N].astype(BF16)
        back_real = (mm(cosine, grid_real) + mm(minus, grid_imag)).astype(BF16)
        back_imag = (mm(cosine, grid_imag) + mm(sine, grid_real)).astype(BF16)
        coil_real = mm(back_real, cosine) + mm(back_imag, minus)
        coil_imag = mm(back_imag, cosine) + mm(back_real, sine)
        for part, field in enumerate(
            (
                map_real * coil_real + map_imag * coil_imag,
                map_real * coil_imag - map_imag * coil_real,
            )
        ):
            shards = field.reshape(coils, height, N)
            adjoint[:, part] = shards
            part_out[step, :, part] = shards.astype(BF16)

        cross = {}
        ring = {}
        for k in RING_FAR + (0,):
            for far in CROSS_FAR:
                cross[far, k] = send(
                    part_out.at[step, cross_x(far) * RING + lax.rem(my_z + k, RING)],
                    part_in.at[step, far, k],
                    cross_send.at[2 * step + 1, far, k],
                    cross_recv.at[2 * step + 1, far, k],
                    {"coil": cross_coil(far)},
                )
        if step == ITERS - 1:
            for copy in mis_cross:
                copy.wait_recv()
            mis_sum = mis_out[...]
            for far in CROSS_FAR:
                mis_sum = mis_sum + mis_in[far]
            mis_mid[...] = mis_sum
            mis_ring = [
                send(
                    mis_mid,
                    mis_end.at[k],
                    mis_send.at[1, k],
                    mis_recv.at[1, k],
                    {"coil": ring_coil(k)},
                )
                for k in RING_FAR
            ]
        for k in RING_FAR + (0,):
            pieces = adjoint[ring_coil(k)]
            for far in CROSS_FAR:
                cross[far, k].wait_recv()
                pieces = pieces + part_in[step, far, k].astype(F32)
            if k:
                mid_out[step, k] = pieces.astype(BF16)
                ring[k] = send(
                    mid_out.at[step, k],
                    mid_in.at[step, k],
                    ring_send.at[2 * step + 1, k],
                    ring_recv.at[2 * step + 1, k],
                    {"coil": ring_coil(k)},
                )
        for copy in sides:
            copy.wait_recv()
        here = (current[step, 0], current[step, 1])
        early = (beside[step, 0, 0], beside[step, 0, 1])
        late = (beside[step, 1, 0], beside[step, 1, 1])
        first = slope(here, early)
        second = slope(late, here)
        for k in RING_FAR:
            ring[k].wait_recv()
            pieces = pieces + mid_in[step, k].astype(F32)
        result = [
            here[part]
            - step_size * (pieces[part] + tv_weight * (first[part] - second[part]))
            for part in range(2)
        ]
        result = wavelet_prox(result[0], result[1], step_size * shrink_weight)
        for part in range(2):
            if step < ITERS - 1:
                current[step + 1, part] = result[part]
                low[step + 1, part] = result[part].astype(BF16)
            else:
                out_ref[:, part, :] = result[part]

    for copy in mis_ring:
        copy.wait_recv()
    for k in RING_FAR:
        mis_sum = mis_sum + mis_end[k]
    mis_sum = jnp.sum(mis_sum, axis=1, keepdims=True) * (0.5 / (coils * NB * BS))
    lane = lax.broadcasted_iota(jnp.int32, (1, ITERS), 1)
    misfit_ref[...] = jnp.where(lane == 0, mis_sum[0:1], mis_sum[1:2])
    for copy in leaving:
        copy.wait_send()


def solution(mesh):
    coils = mesh.shape["coil"]
    frames = mesh.shape["frame"]
    columns = coils // RING
    height = N // coils
    tables = dft_tables()
    vmem = pl.BlockSpec(memory_space=pltpu.VMEM)
    hbm = pl.BlockSpec(memory_space=pltpu.HBM)

    def on_device(
        initial_image,
        coil_maps,
        samples,
        blocks_used,
        row_offset,
        col_offset,
        row_first,
        col_first,
        row_taps,
        col_taps,
    ):
        image, misfit = pl.pallas_call(
            functools.partial(kernel, coils, frames),
            out_shape=(
                jax.ShapeDtypeStruct((height, 2, N), F32),
                jax.ShapeDtypeStruct((1, ITERS), F32),
            ),
            in_specs=[hbm] * 11,
            out_specs=(vmem, vmem),
            scratch_shapes=[
                pltpu.VMEM((height, 2, N), F32),
                pltpu.VMEM((2, N, N), BF16),
                pltpu.VMEM((NB, 2, BS), BF16),
                pltpu.SMEM((1,), jnp.int32),
                pltpu.SMEM((1, NB), jnp.int32),
                pltpu.SMEM((1, NB), jnp.int32),
                pltpu.VMEM((NB, 1, BS), jnp.int32),
                pltpu.VMEM((NB, 1, BS), jnp.int32),
                pltpu.VMEM((NB, KW, BS), BF16),
                pltpu.VMEM((NB, KW, BS), BF16),
                pltpu.VMEM((3, N, N), BF16),
                pltpu.VMEM((ITERS, 2, height, N), F32),
                pltpu.VMEM((ITERS, 2, height, N), BF16),
                pltpu.VMEM((ITERS, coils, 2, height, N), BF16),
                pltpu.VMEM((ITERS, 2, 2, height, N), F32),
                pltpu.VMEM((coils, 2, height, N), F32),
                pltpu.VMEM((ITERS, coils, 2, height, N), BF16),
                pltpu.VMEM((ITERS, columns, RING, 2, height, N), BF16),
                pltpu.VMEM((ITERS, RING, 2, height, N), BF16),
                pltpu.VMEM((ITERS, RING, 2, height, N), BF16),
                pltpu.VMEM((ITERS, BS), F32),
                pltpu.VMEM((columns, ITERS, BS), F32),
                pltpu.VMEM((ITERS, BS), F32),
                pltpu.VMEM((RING, ITERS, BS), F32),
                pltpu.VMEM((NB, N, BS), BF16),
                pltpu.VMEM((NB, N, BS), BF16),
                pltpu.VMEM((2 * N, N), BF16),
                pltpu.VMEM((NB, 2 * N, BS), BF16),
                pltpu.SemaphoreType.DMA((11,)),
                pltpu.SemaphoreType.DMA((2 * ITERS, RING)),
                pltpu.SemaphoreType.DMA((2 * ITERS, RING)),
                pltpu.SemaphoreType.DMA((2 * ITERS, columns, RING)),
                pltpu.SemaphoreType.DMA((2 * ITERS, columns, RING)),
                pltpu.SemaphoreType.DMA((ITERS, 2)),
                pltpu.SemaphoreType.DMA((ITERS, 2)),
                pltpu.SemaphoreType.DMA((2, RING)),
                pltpu.SemaphoreType.DMA((2, RING)),
            ],
            compiler_params=pltpu.CompilerParams(
                collective_id=0, has_side_effects=True, vmem_limit_bytes=67043328
            ),
        )(
            initial_image[:, 0],
            coil_maps[0],
            samples[0, 0],
            blocks_used,
            row_offset,
            col_offset,
            row_first[0][:, None],
            col_first[0][:, None],
            row_taps[0],
            col_taps[0],
            tables,
        )
        return image[:, None], misfit.T

    placed = (
        P("coil", "frame", None, None),
        P("coil", None, None, None),
        P("coil", "frame", None, None, None),
        P("frame"),
        P("frame", None),
        P("frame", None),
        P("frame", None, None),
        P("frame", None, None),
        P("frame", None, None, None),
        P("frame", None, None, None),
    )
    return jax.shard_map(
        on_device,
        mesh=mesh,
        in_specs=placed,
        out_specs=(P("coil", "frame", None, None), P(None, "frame")),
        check_vma=False,
    )
```

time: 80.7 us -> 63.2 us (0.78)
  the two profiles are of different devices: /device:TPU:32 before, /device:TPU:24 now
where the time goes in v1:
time: 63.2 us; the launch traced here: 63 us
  Pallas kernels  59.8 us (95%)
  local copies, waits for them, and re-layouts  1.84 us (3%)
  between operations  1.3 us (2%)
    pallas_call x1, Pallas kernels, on_device(): pl.pallas_call(functools.partial(kernel, coils, frames), out_shape=(jax.S...  59.8 us
    unnamed x4, local copies, waits for them, and re-layouts  1.84 us

profile of v1, /device:TPU:24, one launch (start us, length us, event | category | flops | bytes accessed | tf_op | source)
XLA Modules:
  0.0 63.0 jit_solution(1361861022385255370)
XLA Ops:
  1.3 59.8 %shard_map.122 = (f32[8,2,256]{2,1,0:T(2,128)}, f32[1,2]{1,0:T(1,128)}) custom-call(f32[8,2,256]{2,1,0:T(2,128)} %bitcast.17, bf16[2,256,256]{2,1,0:T(8,128)(2,1)} %bitcast.11, bf16[18,2,256]{2,1,0:T(2,128)(2,1)} %bitcast.14, s32[1]{0:T(128)S(6)} %copy.16.used_hbm, s32[1,18]{1,0:T(1,128)} %row_off_hbm.1, s32[1,18]{1,0:T(1,128)} %col_off_hbm.1, ...), custom_call_target="tpu_custom_call" | custom-call | tf_op jit(solution)/shard_map/pallas_call | solution.py:453
  61.1 0.0 copy-start
  61.1 1.3 %copy.17 = f32[8,1,2,256]{3,2,1,0:T(2,128)} copy(f32[8,1,2,256]{3,2,1,0:T(2,128)} %bitcast.18) | data formatting | bytes 32768
  62.5 0.0 copy-done
  62.5 0.5 copy.18
Async XLA Ops:
  61.1 1.3 %copy-start = (f32[1,2]{1,0:T(1,128)S(1)}, f32[1,2]{1,0:T(1,128)}, u32[]{:S(2)}) copy-start(f32[1,2]{1,0:T(1,128)} %get-tuple-element.5) | copy-start | bytes 28

commit v2 on v1

--- a/solution.py
+++ b/solution.py
@@ -23,7 +23,11 @@
 RING = 8
 RING_FAR = (4, 3, 5, 2, 6, 1, 7)
 CROSS_FAR = (2, 1, 3)
-GROUP = 6
+ALL_FAR = sorted(
+    ((far, k) for far in range(4) for k in range(RING) if far or k),
+    key=lambda to: -(min(to[0], 4 - to[0]) + min(to[1], RING - to[1])),
+)
+
 
 MESH = pl.DeviceIdType.MESH
 F32 = jnp.float32
@@ -139,25 +143,18 @@
     adjoint,
     part_out,
     part_in,
-    mid_out,
-    mid_in,
     mis_out,
     mis_in,
-    mis_mid,
-    mis_end,
     wx,
     wy,
     kspace,
     weighted,
+    back,
     local_sem,
-    ring_send,
-    ring_recv,
-    cross_send,
-    cross_recv,
+    all_send,
+    all_recv,
     side_send,
     side_recv,
-    mis_send,
-    mis_recv,
 ):
     me = lax.axis_index("coil")
     frame = lax.axis_index("frame")
@@ -174,6 +171,9 @@
 
     def cross_coil(k):
         return cross_x(k) * RING + my_z
+
+    def any_coil(far, k):
+        return cross_x(far) * RING + lax.rem(my_z + k, RING)
 
     after = lax.rem(frame + 1, frames)
     before = lax.rem(frame + frames - 1, frames)
@@ -234,11 +234,16 @@
         out[b] = taps_of(first_ref[b], off_ref[0, b], taps_ref[b].astype(F32))
         return carry
 
-    for fetch in fetches[1:4]:
-        fetch.wait()
-    lax.fori_loop(
-        0, NB, functools.partial(build, row_first_ref, row_off_ref, row_taps_ref, wx), 0
-    )
+    def build_rows(start, stop):
+        lax.fori_loop(
+            start, stop, functools.partial(build, row_first_ref, row_off_ref, row_taps_ref, wx), 0
+        )
+
+    def build_columns(start, stop):
+        lax.fori_loop(
+            start, stop, functools.partial(build, col_first_ref, col_off_ref, col_taps_ref, wy), 0
+        )
+
     pl.semaphore_wait(barrier, RING - 1 + columns - 1 + 2)
 
     for step in range(ITERS):
@@ -252,42 +257,59 @@
             )
             for slot, side in ((0, after), (1, before))
         ]
-        ring = {}
-        cross = {}
-        for k in RING_FAR:
-            ring[k] = send(
-                low.at[step],
-                gathered.at[step, me],
-                ring_send.at[2 * step, k],
-                ring_recv.at[2 * step, k],
-                {"coil": ring_coil(k)},
-            )
-
-        def forward(k, source):
-            for far in CROSS_FAR:
-                cross[far, k] = send(
-                    source,
-                    gathered.at[step, my_x * RING + lax.rem(my_z + RING - k, RING)],
-                    cross_send.at[2 * step, far, k],
-                    cross_recv.at[2 * step, far, k],
-                    {"coil": cross_coil(far)},
-                )
-
-        forward(0, low.at[step])
         gathered[step, me] = low[step]
         if step == 0:
-            for fetch in fetches[4:7]:
+            ring = {}
+            cross = []
+            for k in RING_FAR:
+                ring[k] = send(
+                    low.at[step],
+                    gathered.at[step, me],
+                    all_send.at[2 * step, 0, k],
+                    all_recv.at[2 * step, 0, k],
+                    {"coil": ring_coil(k)},
+                )
+
+            def forward(k, source):
+                for far in CROSS_FAR:
+                    copy = send(
+                        source,
+                        gathered.at[step, ring_coil(RING - k)],
+                        all_send.at[2 * step, far, k],
+                        all_recv.at[2 * step, far, k],
+                        {"coil": cross_coil(far)},
+                    )
+                    cross.append(copy)
+
+            forward(0, low.at[step])
+            for fetch in fetches[1:7]:
                 fetch.wait()
-            lax.fori_loop(
-                0, NB, functools.partial(build, col_first_ref, col_off_ref, col_taps_ref, wy), 0
-            )
+            build_rows(0, NB)
+            build_columns(0, NB // 3)
+            for k in reversed(RING_FAR):
+                if k == 6:
+                    build_columns(NB // 3, NB - NB // 3)
+                if k == 5:
+                    build_columns(NB - NB // 3, NB)
+                ring[k].wait_recv()
+                forward(k, gathered.at[step, ring_coil(RING - k)])
             for fetch in fetches[7:]:
                 fetch.wait()
-        for k in reversed(RING_FAR):
-            ring[k].wait_recv()
-            forward(k, gathered.at[step, my_x * RING + lax.rem(my_z + RING - k, RING)])
-        for copy in cross.values():
-            copy.wait_recv()
+            for copy in cross:
+                copy.wait_recv()
+        else:
+            copies = [
+                send(
+                    low.at[step],
+                    gathered.at[step, me],
+                    all_send.at[2 * step, far, k],
+                    all_recv.at[2 * step, far, k],
+                    {"coil": any_coil(far, k)},
+                )
+                for far, k in ALL_FAR
+            ]
+            for copy in copies:
+                copy.wait_recv()
 
         cosine, sine, minus = table_ref[0], table_ref[1], table_ref[2]
         map_real = maps_ref[0].astype(F32)
@@ -302,99 +324,74 @@
         kspace[N : 2 * N] = (mm(half_imag, cosine) + mm(half_real, minus)).astype(BF16)
 
         def visit(b, misfit):
-            across = mm(kspace[...], wy[b])
             rows = wx[b]
             wide = rows.astype(F32)
             measured = samples_ref[b].astype(F32)
             active = jnp.full((1, BS), b, jnp.int32) < used_ref[0]
             for part in range(2):
-                predicted = jnp.sum(across[part * N : part * N + N] * wide, axis=0, keepdims=True)
+                across = mm(kspace[part * N : part * N + N], wy[b])
+                predicted = jnp.sum(across * wide, axis=0, keepdims=True)
                 resid = jnp.where(active, predicted - measured[part : part + 1], 0.0)
                 misfit = misfit + resid * resid
                 weighted[b, part * N : part * N + N] = resid.astype(BF16) * rows
             return misfit
 
-        def visits(group, misfit):
-            for b in range(GROUP):
-                misfit = visit(group * GROUP + b, misfit)
-            return misfit
-
-        misfit = lax.fori_loop(0, NB // GROUP, visits, jnp.zeros((1, BS), F32))
+        misfit = jnp.zeros((1, BS), F32)
+        for b in range(NB):
+            misfit = visit(b, misfit)
         mis_out[step : step + 1, :] = misfit
 
         if step == ITERS - 1:
-            mis_cross = [
+            mis_copies = [
                 send(
                     mis_out,
-                    mis_in.at[far],
-                    mis_send.at[0, far],
-                    mis_recv.at[0, far],
-                    {"coil": cross_coil(far)},
+                    mis_in.at[far, k],
+                    all_send.at[2 * ITERS, far, k],
+                    all_recv.at[2 * ITERS, far, k],
+                    {"coil": any_coil(far, k)},
                 )
-                for far in CROSS_FAR
+                for far, k in ALL_FAR
             ]
 
-        total = mm_nt(weighted[0], wy[0])
-        for b in range(1, NB):
-            total = total + mm_nt(weighted[b], wy[b])
-        grid_real = total[0:N].astype(BF16)
-        grid_imag = total[N : 2 * N].astype(BF16)
-        back_real = (mm(cosine, grid_real) + mm(minus, grid_imag)).astype(BF16)
-        back_imag = (mm(cosine, grid_imag) + mm(sine, grid_real)).astype(BF16)
-        coil_real = mm(back_real, cosine) + mm(back_imag, minus)
-        coil_imag = mm(back_imag, cosine) + mm(back_real, sine)
-        for part, field in enumerate(
-            (
-                map_real * coil_real + map_imag * coil_imag,
-                map_real * coil_imag - map_imag * coil_real,
-            )
-        ):
-            shards = field.reshape(coils, height, N)
-            adjoint[:, part] = shards
-            part_out[step, :, part] = shards.astype(BF16)
-
-        cross = {}
-        ring = {}
-        for k in RING_FAR + (0,):
-            for far in CROSS_FAR:
-                cross[far, k] = send(
-                    part_out.at[step, cross_x(far) * RING + lax.rem(my_z + k, RING)],
-                    part_in.at[step, far, k],
-                    cross_send.at[2 * step + 1, far, k],
-                    cross_recv.at[2 * step + 1, far, k],
-                    {"coil": cross_coil(far)},
+        totals = []
+        for part in range(2):
+            total = mm_nt(weighted[0, part * N : part * N + N], wy[0])
+            for b in range(1, NB):
+                total = total + mm_nt(weighted[b, part * N : part * N + N], wy[b])
+            totals.append(total.astype(BF16))
+        grid_real, grid_imag = totals
+        back[0] = (mm(cosine, grid_real) + mm(minus, grid_imag)).astype(BF16)
+        back[1] = (mm(cosine, grid_imag) + mm(sine, grid_real)).astype(BF16)
+        copies = []
+        for far in CROSS_FAR + (0,):
+            strip = pl.ds(pl.multiple_of(cross_x(far) * RING * height, RING * height), RING * height)
+            back_real, back_imag = back[0, strip], back[1, strip]
+            map_real = maps_ref[0, strip].astype(F32)
+            map_imag = maps_ref[1, strip].astype(F32)
+            coil_real = mm(back_real, cosine) + mm(back_imag, minus)
+            coil_imag = mm(back_imag, cosine) + mm(back_real, sine)
+            for part, field in enumerate(
+                (
+                    map_real * coil_real + map_imag * coil_imag,
+                    map_real * coil_imag - map_imag * coil_real,
                 )
-        if step == ITERS - 1:
-            for copy in mis_cross:
-                copy.wait_recv()
-            mis_sum = mis_out[...]
-            for far in CROSS_FAR:
-                mis_sum = mis_sum + mis_in[far]
-            mis_mid[...] = mis_sum
-            mis_ring = [
-                send(
-                    mis_mid,
-                    mis_end.at[k],
-                    mis_send.at[1, k],
-                    mis_recv.at[1, k],
-                    {"coil": ring_coil(k)},
-                )
-                for k in RING_FAR
-            ]
-        for k in RING_FAR + (0,):
-            pieces = adjoint[ring_coil(k)]
-            for far in CROSS_FAR:
-                cross[far, k].wait_recv()
-                pieces = pieces + part_in[step, far, k].astype(F32)
-            if k:
-                mid_out[step, k] = pieces.astype(BF16)
-                ring[k] = send(
-                    mid_out.at[step, k],
-                    mid_in.at[step, k],
-                    ring_send.at[2 * step + 1, k],
-                    ring_recv.at[2 * step + 1, k],
-                    {"coil": ring_coil(k)},
-                )
+            ):
+                shards = field.reshape(RING, height, N)
+                part_out[step, far, :, part] = shards.astype(BF16)
+                if far == 0:
+                    adjoint[:, part] = shards
+            for k in RING_FAR + (0,):
+                if far or k:
+                    copies.append(
+                        send(
+                            part_out.at[step, far, lax.rem(my_z + k, RING)],
+                            part_in.at[step, far, k],
+                            all_send.at[2 * step + 1, far, k],
+                            all_recv.at[2 * step + 1, far, k],
+                            {"coil": any_coil(far, k)},
+                        )
+                    )
+
         for copy in sides:
             copy.wait_recv()
         here = (current[step, 0], current[step, 1])
@@ -402,9 +399,13 @@
         late = (beside[step, 1, 0], beside[step, 1, 1])
         first = slope(here, early)
         second = slope(late, here)
-        for k in RING_FAR:
-            ring[k].wait_recv()
-            pieces = pieces + mid_in[step, k].astype(F32)
+        pieces = adjoint[my_z]
+        for copy in copies:
+            copy.wait_recv()
+        for far in range(columns):
+            for k in range(RING):
+                if far or k:
+                    pieces = pieces + part_in[step, far, k].astype(F32)
         result = [
             here[part]
             - step_size * (pieces[part] + tv_weight * (first[part] - second[part]))
@@ -418,10 +419,11 @@
             else:
                 out_ref[:, part, :] = result[part]
 
-    for copy in mis_ring:
+    mis_sum = mis_out[...]
+    for copy in mis_copies:
         copy.wait_recv()
-    for k in RING_FAR:
-        mis_sum = mis_sum + mis_end[k]
+    for far, k in ALL_FAR:
+        mis_sum = mis_sum + mis_in[far, k]
     mis_sum = jnp.sum(mis_sum, axis=1, keepdims=True) * (0.5 / (coils * NB * BS))
     lane = lax.broadcasted_iota(jnp.int32, (1, ITERS), 1)
     misfit_ref[...] = jnp.where(lane == 0, mis_sum[0:1], mis_sum[1:2])
@@ -474,28 +476,21 @@
                 pltpu.VMEM((ITERS, 2, height, N), BF16),
                 pltpu.VMEM((ITERS, coils, 2, height, N), BF16),
                 pltpu.VMEM((ITERS, 2, 2, height, N), F32),
-                pltpu.VMEM((coils, 2, height, N), F32),
-                pltpu.VMEM((ITERS, coils, 2, height, N), BF16),
+                pltpu.VMEM((RING, 2, height, N), F32),
                 pltpu.VMEM((ITERS, columns, RING, 2, height, N), BF16),
-                pltpu.VMEM((ITERS, RING, 2, height, N), BF16),
-                pltpu.VMEM((ITERS, RING, 2, height, N), BF16),
+                pltpu.VMEM((ITERS, columns, RING, 2, height, N), BF16),
                 pltpu.VMEM((ITERS, BS), F32),
-                pltpu.VMEM((columns, ITERS, BS), F32),
-                pltpu.VMEM((ITERS, BS), F32),
-                pltpu.VMEM((RING, ITERS, BS), F32),
+                pltpu.VMEM((columns, RING, ITERS, BS), F32),
                 pltpu.VMEM((NB, N, BS), BF16),
                 pltpu.VMEM((NB, N, BS), BF16),
                 pltpu.VMEM((2 * N, N), BF16),
                 pltpu.VMEM((NB, 2 * N, BS), BF16),
+                pltpu.VMEM((2, N, N), BF16),
                 pltpu.SemaphoreType.DMA((11,)),
-                pltpu.SemaphoreType.DMA((2 * ITERS, RING)),
-                pltpu.SemaphoreType.DMA((2 * ITERS, RING)),
-                pltpu.SemaphoreType.DMA((2 * ITERS, columns, RING)),
-                pltpu.SemaphoreType.DMA((2 * ITERS, columns, RING)),
+                pltpu.SemaphoreType.DMA((2 * ITERS + 1, columns, RING)),
+                pltpu.SemaphoreType.DMA((2 * ITERS + 1, columns, RING)),
                 pltpu.SemaphoreType.DMA((ITERS, 2)),
                 pltpu.SemaphoreType.DMA((ITERS, 2)),
-                pltpu.SemaphoreType.DMA((2, RING)),
-                pltpu.SemaphoreType.DMA((2, RING)),
             ],
             compiler_params=pltpu.CompilerParams(
                 collective_id=0, has_side_effects=True, vmem_limit_bytes=67043328

time: 63.2 us -> 59 us (0.934)
  Pallas kernels: 59.8 us -> 55.7 us
    pallas_call x1, Pallas kernels: 59.8 us -> 55.7 us  [on_device(): pl.pallas_call(functools.partial(kernel, coils, frames), out_shape=(jax.S...]
where the time goes in v2:
time: 59 us; the launch traced here: 58.8 us
  Pallas kernels  55.7 us (94%)
  local copies, waits for them, and re-layouts  1.84 us (3%)
  between operations  1.3 us (2%)
    pallas_call x1, Pallas kernels, on_device(): pl.pallas_call(functools.partial(kernel, coils, frames), out_shape=(jax.S...  55.7 us
    unnamed x4, local copies, waits for them, and re-layouts  1.84 us

profile of v2, /device:TPU:24, one launch (start us, length us, event | category | flops | bytes accessed | tf_op | source)
XLA Modules:
  0.0 58.8 jit_solution(3443719834466973127)
XLA Ops:
  1.3 55.7 %shard_map.122 = (f32[8,2,256]{2,1,0:T(2,128)}, f32[1,2]{1,0:T(1,128)}) custom-call(f32[8,2,256]{2,1,0:T(2,128)} %bitcast.17, bf16[2,256,256]{2,1,0:T(8,128)(2,1)} %bitcast.11, bf16[18,2,256]{2,1,0:T(2,128)(2,1)} %bitcast.14, s32[1]{0:T(128)S(6)} %copy.16.used_hbm, s32[1,18]{1,0:T(1,128)} %row_off_hbm.1, s32[1,18]{1,0:T(1,128)} %col_off_hbm.1, ...), custom_call_target="tpu_custom_call" | custom-call | tf_op jit(solution)/shard_map/pallas_call | solution.py:455
  57.0 0.0 copy-start
  57.0 1.3 %copy.17 = f32[8,1,2,256]{3,2,1,0:T(2,128)} copy(f32[8,1,2,256]{3,2,1,0:T(2,128)} %bitcast.18) | data formatting | bytes 32768
  58.3 0.0 copy-done
  58.3 0.5 copy.18
Async XLA Ops:
  57.0 1.3 %copy-start = (f32[1,2]{1,0:T(1,128)S(1)}, f32[1,2]{1,0:T(1,128)}, u32[]{:S(2)}) copy-start(f32[1,2]{1,0:T(1,128)} %get-tuple-element.5) | copy-start | bytes 28

commit v3 on v2

--- a/solution.py
+++ b/solution.py
@@ -145,6 +145,8 @@
     part_in,
     mis_out,
     mis_in,
+    mis_mid,
+    mis_end,
     wx,
     wy,
     kspace,
@@ -155,6 +157,8 @@
     all_recv,
     side_send,
     side_recv,
+    mis_send,
+    mis_recv,
 ):
     me = lax.axis_index("coil")
     frame = lax.axis_index("frame")
@@ -342,15 +346,15 @@
         mis_out[step : step + 1, :] = misfit
 
         if step == ITERS - 1:
-            mis_copies = [
+            mis_cross = [
                 send(
                     mis_out,
-                    mis_in.at[far, k],
-                    all_send.at[2 * ITERS, far, k],
-                    all_recv.at[2 * ITERS, far, k],
-                    {"coil": any_coil(far, k)},
+                    mis_in.at[far],
+                    mis_send.at[0, far],
+                    mis_recv.at[0, far],
+                    {"coil": cross_coil(far)},
                 )
-                for far, k in ALL_FAR
+                for far in CROSS_FAR
             ]
 
         totals = []
@@ -392,6 +396,23 @@
                         )
                     )
 
+        if step == ITERS - 1:
+            for copy in mis_cross:
+                copy.wait_recv()
+            mis_sum = mis_out[...]
+            for far in CROSS_FAR:
+                mis_sum = mis_sum + mis_in[far]
+            mis_mid[...] = mis_sum
+            mis_ring = [
+                send(
+                    mis_mid,
+                    mis_end.at[k],
+                    mis_send.at[1, k],
+                    mis_recv.at[1, k],
+                    {"coil": ring_coil(k)},
+                )
+                for k in RING_FAR
+            ]
         for copy in sides:
             copy.wait_recv()
         here = (current[step, 0], current[step, 1])
@@ -419,11 +440,10 @@
             else:
                 out_ref[:, part, :] = result[part]
 
-    mis_sum = mis_out[...]
-    for copy in mis_copies:
+    for copy in mis_ring:
         copy.wait_recv()
-    for far, k in ALL_FAR:
-        mis_sum = mis_sum + mis_in[far, k]
+    for k in RING_FAR:
+        mis_sum = mis_sum + mis_end[k]
     mis_sum = jnp.sum(mis_sum, axis=1, keepdims=True) * (0.5 / (coils * NB * BS))
     lane = lax.broadcasted_iota(jnp.int32, (1, ITERS), 1)
     misfit_ref[...] = jnp.where(lane == 0, mis_sum[0:1], mis_sum[1:2])
@@ -455,8 +475,8 @@
         image, misfit = pl.pallas_call(
             functools.partial(kernel, coils, frames),
             out_shape=(
-                jax.ShapeDtypeStruct((height, 2, N), F32),
-                jax.ShapeDtypeStruct((1, ITERS), F32),
+                pltpu.VMEM((height, 2, N), F32),
+                pltpu.VMEM((1, ITERS), F32),
             ),
             in_specs=[hbm] * 11,
             out_specs=(vmem, vmem),
@@ -480,20 +500,24 @@
                 pltpu.VMEM((ITERS, columns, RING, 2, height, N), BF16),
                 pltpu.VMEM((ITERS, columns, RING, 2, height, N), BF16),
                 pltpu.VMEM((ITERS, BS), F32),
-                pltpu.VMEM((columns, RING, ITERS, BS), F32),
+                pltpu.VMEM((columns, ITERS, BS), F32),
+                pltpu.VMEM((ITERS, BS), F32),
+                pltpu.VMEM((RING, ITERS, BS), F32),
                 pltpu.VMEM((NB, N, BS), BF16),
                 pltpu.VMEM((NB, N, BS), BF16),
                 pltpu.VMEM((2 * N, N), BF16),
                 pltpu.VMEM((NB, 2 * N, BS), BF16),
                 pltpu.VMEM((2, N, N), BF16),
                 pltpu.SemaphoreType.DMA((11,)),
-                pltpu.SemaphoreType.DMA((2 * ITERS + 1, columns, RING)),
-                pltpu.SemaphoreType.DMA((2 * ITERS + 1, columns, RING)),
+                pltpu.SemaphoreType.DMA((2 * ITERS, columns, RING)),
+                pltpu.SemaphoreType.DMA((2 * ITERS, columns, RING)),
                 pltpu.SemaphoreType.DMA((ITERS, 2)),
                 pltpu.SemaphoreType.DMA((ITERS, 2)),
+                pltpu.SemaphoreType.DMA((2, RING)),
+                pltpu.SemaphoreType.DMA((2, RING)),
             ],
             compiler_params=pltpu.CompilerParams(
-                collective_id=0, has_side_effects=True, vmem_limit_bytes=67043328
+                collective_id=0, has_side_effects=True, vmem_limit_bytes=67043328 - 32 * 1024
             ),
         )(
             initial_image[:, 0],

time: 59 us -> 57 us (0.966)
  Pallas kernels: 55.7 us -> 54.4 us
  local copies, waits for them, and re-layouts: 1.84 us -> 1.12 us
    pallas_call x1, Pallas kernels: 55.7 us -> 54.4 us  [on_device(): pl.pallas_call(functools.partial(kernel, coils, frames), out_shape=(pltpu...]
    unnamed x4 -> x2, local copies, waits for them, and re-layouts: 1.84 us -> 1.12 us
where the time goes in v3:
time: 57 us; the launch traced here: 56.8 us
  Pallas kernels  54.4 us (95%)
  between operations  1.29 us (2%)
  local copies, waits for them, and re-layouts  1.12 us (2%)
    pallas_call x1, Pallas kernels, on_device(): pl.pallas_call(functools.partial(kernel, coils, frames), out_shape=(pltpu...  54.4 us

profile of v3, /device:TPU:24, one launch (start us, length us, event | category | flops | bytes accessed | tf_op | source)
XLA Modules:
  0.0 56.8 jit_solution(709243788588846355)
XLA Ops:
  1.3 54.4 %shard_map.122 = (f32[8,2,256]{2,1,0:T(2,128)S(1)}, f32[1,2]{1,0:T(1,128)S(1)}) custom-call(f32[8,2,256]{2,1,0:T(2,128)} %bitcast.19, bf16[2,256,256]{2,1,0:T(8,128)(2,1)} %bitcast.13, bf16[18,2,256]{2,1,0:T(2,128)(2,1)} %bitcast.16, s32[1]{0:T(128)S(6)} %copy.18.used_hbm, s32[1,18]{1,0:T(1,128)} %row_off_hbm.1, s32[1,18]{1,0:T(1,128)} %col_off_hbm.1, ...), custom_call_target="tpu_custom_call" | custom-call | tf_op jit(solution)/shard_map/pallas_call | solution.py:475
  55.7 0.6 %copy.16 = f32[8,1,2,256]{3,2,1,0:T(2,128)} copy(f32[8,1,2,256]{3,2,1,0:T(2,128)S(1)} %bitcast.11) | data formatting | bytes 32768
  56.3 0.5 copy.17

commit v4 on v3

--- a/solution.py
+++ b/solution.py
@@ -21,6 +21,7 @@
 shrink_weight = 0.1
 
 RING = 8
+EARLY = 11
 RING_FAR = (4, 3, 5, 2, 6, 1, 7)
 CROSS_FAR = (2, 1, 3)
 ALL_FAR = sorted(
@@ -216,6 +217,11 @@
 
     leaving = []
 
+    def drain():
+        for copy in leaving:
+            copy.wait_send()
+        leaving.clear()
+
     def send(source, target, send_sem, recv_sem, device):
         copy = pltpu.make_async_remote_copy(
             src_ref=source,
@@ -248,6 +254,9 @@
             start, stop, functools.partial(build, col_first_ref, col_off_ref, col_taps_ref, wy), 0
         )
 
+    for fetch in fetches[1:4]:
+        fetch.wait()
+    build_rows(0, EARLY)
     pl.semaphore_wait(barrier, RING - 1 + columns - 1 + 2)
 
     for step in range(ITERS):
@@ -263,15 +272,24 @@
         ]
         gathered[step, me] = low[step]
         if step == 0:
-            ring = {}
             cross = []
             for k in RING_FAR:
-                ring[k] = send(
+                send(
                     low.at[step],
                     gathered.at[step, me],
                     all_send.at[2 * step, 0, k],
                     all_recv.at[2 * step, 0, k],
                     {"coil": ring_coil(k)},
+                )
+
+            def arrival(k):
+                return pltpu.make_async_remote_copy(
+                    src_ref=low.at[step],
+                    dst_ref=gathered.at[step, ring_coil(RING - k)],
+                    send_sem=all_send.at[2 * step, 0, k],
+                    recv_sem=all_recv.at[2 * step, 0, k],
+                    device_id={"coil": ring_coil(k)},
+                    device_id_type=MESH,
                 )
 
             def forward(k, source):
@@ -286,17 +304,15 @@
                     cross.append(copy)
 
             forward(0, low.at[step])
-            for fetch in fetches[1:7]:
+            for fetch in fetches[4:7]:
                 fetch.wait()
-            build_rows(0, NB)
-            build_columns(0, NB // 3)
-            for k in reversed(RING_FAR):
-                if k == 6:
-                    build_columns(NB // 3, NB - NB // 3)
-                if k == 5:
-                    build_columns(NB - NB // 3, NB)
-                ring[k].wait_recv()
-                forward(k, gathered.at[step, ring_coil(RING - k)])
+            build_rows(EARLY, NB)
+            build_columns(0, NB)
+            for place in range(RING - 1):
+                sender = place + (my_z <= place).astype(jnp.int32)
+                k = lax.rem(my_z + RING - sender, RING)
+                arrival(k).wait_recv()
+                forward(k, gathered.at[step, my_x * RING + sender])
             for fetch in fetches[7:]:
                 fetch.wait()
             for copy in cross:
@@ -312,6 +328,7 @@
                 )
                 for far, k in ALL_FAR
             ]
+            drain()
             for copy in copies:
                 copy.wait_recv()
 
@@ -367,11 +384,18 @@
         back[0] = (mm(cosine, grid_real) + mm(minus, grid_imag)).astype(BF16)
         back[1] = (mm(cosine, grid_imag) + mm(sine, grid_real)).astype(BF16)
         copies = []
-        for far in CROSS_FAR + (0,):
-            strip = pl.ds(pl.multiple_of(cross_x(far) * RING * height, RING * height), RING * height)
-            back_real, back_imag = back[0, strip], back[1, strip]
-            map_real = maps_ref[0, strip].astype(F32)
-            map_imag = maps_ref[1, strip].astype(F32)
+        for pair in ((2, 1), (3, 0)):
+            strips = [
+                pl.ds(pl.multiple_of(cross_x(far) * RING * height, RING * height), RING * height)
+                for far in pair
+            ]
+
+            def taken(ref, part):
+                return jnp.concatenate([ref[part, strip] for strip in strips], axis=0)
+
+            back_real, back_imag = taken(back, 0), taken(back, 1)
+            map_real = taken(maps_ref, 0).astype(F32)
+            map_imag = taken(maps_ref, 1).astype(F32)
             coil_real = mm(back_real, cosine) + mm(back_imag, minus)
             coil_imag = mm(back_imag, cosine) + mm(back_real, sine)
             for part, field in enumerate(
@@ -380,21 +404,23 @@
                     map_real * coil_imag - map_imag * coil_real,
                 )
             ):
-                shards = field.reshape(RING, height, N)
-                part_out[step, far, :, part] = shards.astype(BF16)
-                if far == 0:
-                    adjoint[:, part] = shards
-            for k in RING_FAR + (0,):
-                if far or k:
-                    copies.append(
-                        send(
-                            part_out.at[step, far, lax.rem(my_z + k, RING)],
-                            part_in.at[step, far, k],
-                            all_send.at[2 * step + 1, far, k],
-                            all_recv.at[2 * step + 1, far, k],
-                            {"coil": any_coil(far, k)},
+                shards = field.reshape(2, RING, height, N)
+                for place, far in enumerate(pair):
+                    part_out[step, far, :, part] = shards[place].astype(BF16)
+                    if far == 0:
+                        adjoint[:, part] = shards[place]
+            for far in pair:
+                for k in RING_FAR + (0,):
+                    if far or k:
+                        copies.append(
+                            send(
+                                part_out.at[step, far, lax.rem(my_z + k, RING)],
+                                part_in.at[step, far, k],
+                                all_send.at[2 * step + 1, far, k],
+                                all_recv.at[2 * step + 1, far, k],
+                                {"coil": any_coil(far, k)},
+                            )
                         )
-                    )
 
         if step == ITERS - 1:
             for copy in mis_cross:
@@ -447,8 +473,7 @@
     mis_sum = jnp.sum(mis_sum, axis=1, keepdims=True) * (0.5 / (coils * NB * BS))
     lane = lax.broadcasted_iota(jnp.int32, (1, ITERS), 1)
     misfit_ref[...] = jnp.where(lane == 0, mis_sum[0:1], mis_sum[1:2])
-    for copy in leaving:
-        copy.wait_send()
+    drain()
 
 
 def solution(mesh):

time: 57 us -> 56.1 us (0.984)
  Pallas kernels: 54.4 us -> 53.5 us
    pallas_call x1, Pallas kernels: 54.4 us -> 53.5 us  [on_device(): pl.pallas_call(functools.partial(kernel, coils, frames), out_shape=(pltpu...]
where the time goes in v4:
time: 56.1 us; the launch traced here: 55.9 us
  Pallas kernels  53.5 us (95%)
  between operations  1.29 us (2%)
  local copies, waits for them, and re-layouts  1.12 us (2%)
    pallas_call x1, Pallas kernels, on_device(): pl.pallas_call(functools.partial(kernel, coils, frames), out_shape=(pltpu...  53.5 us

profile of v4, /device:TPU:24, one launch (start us, length us, event | category | flops | bytes accessed | tf_op | source)
XLA Modules:
  0.0 55.9 jit_solution(10092112820084905638)
XLA Ops:
  1.3 53.5 %shard_map.122 = (f32[8,2,256]{2,1,0:T(2,128)S(1)}, f32[1,2]{1,0:T(1,128)S(1)}) custom-call(f32[8,2,256]{2,1,0:T(2,128)} %bitcast.19, bf16[2,256,256]{2,1,0:T(8,128)(2,1)} %bitcast.13, bf16[18,2,256]{2,1,0:T(2,128)(2,1)} %bitcast.16, s32[1]{0:T(128)S(6)} %copy.18.used_hbm, s32[1,18]{1,0:T(1,128)} %row_off_hbm.1, s32[1,18]{1,0:T(1,128)} %col_off_hbm.1, ...), custom_call_target="tpu_custom_call" | custom-call | tf_op jit(solution)/shard_map/pallas_call | solution.py:500
  54.8 0.6 %copy.16 = f32[8,1,2,256]{3,2,1,0:T(2,128)} copy(f32[8,1,2,256]{3,2,1,0:T(2,128)S(1)} %bitcast.11) | data formatting | bytes 32768
  55.4 0.5 copy.17

commit v5 on v4

--- a/solution.py
+++ b/solution.py
@@ -307,12 +307,13 @@
             for fetch in fetches[4:7]:
                 fetch.wait()
             build_rows(EARLY, NB)
-            build_columns(0, NB)
+            build_columns(0, NB // 3)
             for place in range(RING - 1):
                 sender = place + (my_z <= place).astype(jnp.int32)
                 k = lax.rem(my_z + RING - sender, RING)
                 arrival(k).wait_recv()
                 forward(k, gathered.at[step, my_x * RING + sender])
+            build_columns(NB // 3, NB)
             for fetch in fetches[7:]:
                 fetch.wait()
             for copy in cross:

time: 56.1 us -> 56.1 us (level)
  no operation moved by 1% of the time
where the time goes in v5:
time: 56.1 us; the launch traced here: 55.9 us
  Pallas kernels  53.5 us (95%)
  between operations  1.29 us (2%)
  local copies, waits for them, and re-layouts  1.12 us (2%)
    pallas_call x1, Pallas kernels, on_device(): pl.pallas_call(functools.partial(kernel, coils, frames), out_shape=(pltpu...  53.5 us

profile of v5, /device:TPU:24, one launch (start us, length us, event | category | flops | bytes accessed | tf_op | source)
XLA Modules:
  0.0 55.9 jit_solution(3259724140555218413)
XLA Ops:
  1.3 53.5 %shard_map.122 = (f32[8,2,256]{2,1,0:T(2,128)S(1)}, f32[1,2]{1,0:T(1,128)S(1)}) custom-call(f32[8,2,256]{2,1,0:T(2,128)} %bitcast.19, bf16[2,256,256]{2,1,0:T(8,128)(2,1)} %bitcast.13, bf16[18,2,256]{2,1,0:T(2,128)(2,1)} %bitcast.16, s32[1]{0:T(128)S(6)} %copy.18.used_hbm, s32[1,18]{1,0:T(1,128)} %row_off_hbm.1, s32[1,18]{1,0:T(1,128)} %col_off_hbm.1, ...), custom_call_target="tpu_custom_call" | custom-call | tf_op jit(solution)/shard_map/pallas_call | solution.py:501
  54.8 0.6 %copy.16 = f32[8,1,2,256]{3,2,1,0:T(2,128)} copy(f32[8,1,2,256]{3,2,1,0:T(2,128)S(1)} %bitcast.11) | data formatting | bytes 32768
  55.4 0.5 copy.17
